TPU v7x, 64 devices: a 2x2x8 block of a 4x4x8 slice. The times are simulated.
64 devices in a mesh: dp: 4 (over x, y), sp: 16 (over z, core).
Axes of the slice: x: 2, y: 2, z: 8, core: 2. Of those that a mesh axis runs over, the one named last changes fastest.
The devices are a block of a 4x4x8 slice.
Arguments:
- image_tokens: bfloat16 [128, 256, 1024], P('dp', 'sp'), parts along dimension 0
- ln1_gain: float32 [2, 1024], replicated
- ln1_shift: float32 [2, 1024], replicated
- w_qkv: bfloat16 [2, 1024, 3, 16, 64], replicated
- b_qkv: float32 [2, 3, 16, 64], replicated
- w_out: bfloat16 [2, 16, 64, 1024], replicated
- b_out: float32 [2, 1024], replicated
- ln2_gain: float32 [2, 1024], replicated
- ln2_shift: float32 [2, 1024], replicated
- w_up: bfloat16 [2, 1024, 4096], replicated
- b_up: float32 [2, 4096], replicated
- w_down: bfloat16 [2, 4096, 1024], replicated
- b_down: float32 [2, 1024], replicated
Outputs:
- output: bfloat16 [128, 256, 1024], P('dp', 'sp'), parts along dimension 0
There are 4 independent parts. A program takes and returns all parts, laid end to end along the dimension named above; an argument that names none is the same for every part.
All inputs are finite; a program needn't handle non-finite values.
Results may differ from a plain program's by a relative error of at most 0.0143029.
Values are sent between devices in bfloat16 or wider.
A program may use at most 768 MiB of HBM per device.

v0:
```python
import functools
import math

import jax
import jax.numpy as jnp
from jax import lax
from jax.experimental import pallas as pl
from jax.experimental.pallas import tpu as pltpu
from jax.sharding import PartitionSpec as P

LN_EPS = 1e-6
MESH = pl.DeviceIdType.MESH
BF = jnp.bfloat16
F32 = jnp.float32
NT = (((1,), (1,)), ((), ()))


def norm_rows(src, dst, gain, shift, rows):
    total = src.shape[0]
    width = src.shape[1]
    for start in range(0, total, rows):
        values = src[pl.ds(start, rows), :].astype(F32)
        mean_val = jnp.sum(values, axis=-1, keepdims=True) * (1.0 / width)
        centred = values - mean_val
        var_val = jnp.sum(centred * centred, axis=-1, keepdims=True) * (1.0 / width)
        dst[pl.ds(start, rows), :] = (centred * lax.rsqrt(var_val + LN_EPS) * gain + shift).astype(BF)


def gelu(x):
    c0 = math.sqrt(2.0 / math.pi)
    c1 = c0 * 0.044715
    return 0.5 * x * (1.0 + jnp.tanh(x * (c0 + c1 * (x * x))))


def kernel(peers, x_ref, g1_hbm, s1_hbm, wqkv_hbm, bqkv_hbm, wout_hbm, bout_hbm, g2_hbm, s2_hbm, wup_hbm, bup_hbm, wdown_hbm, bdown_hbm,
           out_ref,
           hid, wqkv, wout, wup, wdown, g1, s1, bqkv, bout, g2, s2, bup, bdown,
           normed, q_t, v_t, keys, mixed, active,
           w_sem, p_sem, in_send, in_recv, out_send, out_recv):
    images = hid.shape[0]
    block = x_ref.shape[1]
    layers, heads, head_dim = bqkv.shape[0], bqkv.shape[2], bqkv.shape[3]
    tokens, width = hid.shape[1], hid.shape[2]
    mlp_dim = wup.shape[2]
    me = lax.axis_index('sp')

    params = [pltpu.make_async_copy(src, dst, p_sem.at[i]) for i, (src, dst) in enumerate((
        (g1_hbm, g1), (s1_hbm, s1), (bqkv_hbm, bqkv), (bout_hbm, bout), (g2_hbm, g2), (s2_hbm, s2), (bup_hbm, bup), (bdown_hbm, bdown)))]

    def weight_copies(layer):
        return [pltpu.make_async_copy(src.at[layer], dst.at[layer], w_sem.at[layer, i]) for i, (src, dst) in enumerate((
            (wqkv_hbm, wqkv), (wout_hbm, wout), (wup_hbm, wup), (wdown_hbm, wdown)))]

    barrier = pltpu.get_barrier_semaphore()
    for step in range(1, peers):
        pl.semaphore_signal(barrier, inc=1, device_id={'sp': lax.rem(me + step, peers)}, device_id_type=MESH)
    for copy in params:
        copy.start()
    for copy in weight_copies(0):
        copy.start()
    pl.semaphore_wait(barrier, peers - 1)

    order = sorted(range(1, peers), key=lambda s: -min(s // 2, (peers - s) // 2))
    my_rows = pl.ds(pl.multiple_of(me * block, block), block)
    for image in range(images):
        for step in order:
            peer = lax.rem(me + step, peers)
            pltpu.make_async_remote_copy(
                src_ref=x_ref.at[peer * images + image], dst_ref=hid.at[image, my_rows, :],
                send_sem=in_send, recv_sem=in_recv.at[image],
                device_id={'sp': peer}, device_id_type=MESH).start()
        pltpu.make_async_copy(x_ref.at[me * images + image], hid.at[image, my_rows, :], in_recv.at[image]).start()
    for layer in range(1, layers):
        for copy in weight_copies(layer):
            copy.start()
    for copy in params:
        copy.wait()

    def body(step_idx, carry):
        image = step_idx // layers
        layer = lax.rem(step_idx, layers)
        state = hid.at[image]

        def weight_wait(i):
            @pl.when(image == 0)
            def _():
                weight_copies(layer)[i].wait()

        @pl.when(layer == 0)
        def _():
            pltpu.make_async_copy(state, state, in_recv.at[image]).wait()

        row = pl.ds(layer, 1)
        norm_rows(state, normed, g1[row, :], s1[row, :], 32)
        weight_wait(0)

        for slot, dst in ((0, q_t), (2, v_t)):
            bias = bqkv[layer, slot].T
            for start in range(0, width, 512):
                part = lax.dot_general(wqkv[layer, pl.ds(slot * width + start, 512), :], normed[...], NT, preferred_element_type=F32)
                for off in range(0, 512, head_dim):
                    head = (start + off) // head_dim
                    dst[pl.ds(start + off, head_dim), :] = (part[off:off + head_dim] + bias[:, head:head + 1]).astype(BF)
        for start in range(0, width, 512):
            part = lax.dot_general(normed[...], wqkv[layer, pl.ds(width + start, 512), :], NT, preferred_element_type=F32)
            bias = jnp.concatenate([bqkv[layer, 1, pl.ds((start + off) // head_dim, 1), :] for off in range(0, 512, head_dim)], axis=-1)
            keys[:, pl.ds(start, 512)] = (part + bias).astype(BF)

        scale = head_dim ** -0.5 / math.log(2.0)
        zeros = jnp.zeros((head_dim, tokens), BF)
        for pair in range(0, heads, 2):
            cols = pl.ds(pair * head_dim, 2 * head_dim)
            outs = []
            for head in (pair, pair + 1):
                q_head = q_t[pl.ds(head * head_dim, head_dim), :]
                rhs = jnp.concatenate([q_head, zeros] if head == pair else [zeros, q_head], axis=0)
                scores = jnp.dot(keys[:, cols], rhs, preferred_element_type=F32)
                peak = jnp.max(scores, axis=0, keepdims=True)
                prob = jnp.exp2((scores - peak) * scale)
                total = jnp.sum(prob, axis=0, keepdims=True)
                mix = jnp.dot(v_t[pl.ds(head * head_dim, head_dim), :], prob.astype(BF), preferred_element_type=F32)
                outs.append(mix * (1.0 / total))
            mixed[:, cols] = jnp.concatenate(outs, axis=0).T.astype(BF)

        weight_wait(1)
        for start in range(0, width, 512):
            cols = pl.ds(start, 512)
            part = jnp.dot(mixed[...], wout[layer, :, cols], preferred_element_type=F32) + bout[row, cols]
            state[:, cols] = (state[:, cols].astype(F32) + part).astype(BF)

        norm_rows(state, normed, g2[row, :], s2[row, :], 32)
        weight_wait(2)
        for start in range(0, mlp_dim, 512):
            cols = pl.ds(start, 512)
            part = jnp.dot(normed[...], wup[layer, :, cols], preferred_element_type=F32) + bup[row, cols]
            active[:, cols] = gelu(part).astype(BF)
        weight_wait(3)
        for start in range(0, width, 512):
            cols = pl.ds(start, 512)
            part = jnp.dot(active[...], wdown[layer, :, cols], preferred_element_type=F32) + bdown[row, cols]
            state[:, cols] = (state[:, cols].astype(F32) + part).astype(BF)

        @pl.when(layer == layers - 1)
        def _():
            for step in order:
                peer = lax.rem(me + step, peers)
                pltpu.make_async_remote_copy(
                    src_ref=hid.at[image, pl.ds(pl.multiple_of(peer * block, block), block), :],
                    dst_ref=out_ref.at[me * images + image],
                    send_sem=out_send, recv_sem=out_recv,
                    device_id={'sp': peer}, device_id_type=MESH).start()
            pltpu.make_async_copy(hid.at[image, my_rows, :], out_ref.at[me * images + image], out_recv).start()
        return carry

    lax.fori_loop(0, images * layers, body, 0)

    sent = x_ref.at[pl.ds(0, (peers - 1) * images)]
    pltpu.make_async_copy(sent, sent, in_send).wait()
    pltpu.make_async_copy(sent, sent, out_send).wait()
    pltpu.make_async_copy(out_ref, out_ref, out_recv).wait()


def solution(mesh):
    token_spec = P('dp', 'sp', None)
    peers = mesh.shape['sp']

    def device_step(image_tokens, ln1_gain, ln1_shift, w_qkv, b_qkv, w_out, b_out, ln2_gain, ln2_shift, w_up, b_up, w_down, b_down):
        total_images, block, width = image_tokens.shape
        layers, _, _, heads, head_dim = w_qkv.shape
        mlp_dim = w_up.shape[-1]
        images = total_images // peers
        tokens = block * peers
        inner = heads * head_dim
        w_qkv_t = jnp.transpose(w_qkv, (0, 2, 3, 4, 1)).reshape(layers, 3 * inner, width)
        w_out_m = w_out.reshape(layers, inner, width)
        args = (image_tokens, ln1_gain, ln1_shift, w_qkv_t, b_qkv, w_out_m, b_out, ln2_gain, ln2_shift, w_up, b_up, w_down, b_down)
        small = lambda a: pltpu.VMEM(a.shape, a.dtype)
        return pl.pallas_call(
            functools.partial(kernel, peers),
            out_shape=jax.ShapeDtypeStruct(image_tokens.shape, image_tokens.dtype),
            in_specs=[pl.BlockSpec(memory_space=pl.ANY)] * len(args),
            out_specs=pl.BlockSpec(memory_space=pl.ANY),
            scratch_shapes=[
                pltpu.VMEM((images, tokens, width), BF),
                small(w_qkv_t), small(w_out_m), small(w_up), small(w_down),
                small(ln1_gain), small(ln1_shift), small(b_qkv), small(b_out), small(ln2_gain), small(ln2_shift), small(b_up), small(b_down),
                pltpu.VMEM((tokens, width), BF),
                pltpu.VMEM((inner, tokens), BF),
                pltpu.VMEM((inner, tokens), BF),
                pltpu.VMEM((tokens, inner), BF),
                pltpu.VMEM((tokens, inner), BF),
                pltpu.VMEM((tokens, mlp_dim), BF),
                pltpu.SemaphoreType.DMA((layers, 4)),
                pltpu.SemaphoreType.DMA((8,)),
                pltpu.SemaphoreType.DMA,
                pltpu.SemaphoreType.DMA((images,)),
                pltpu.SemaphoreType.DMA,
                pltpu.SemaphoreType.DMA,
            ],
            compiler_params=pltpu.CompilerParams(collective_id=0, has_side_effects=True, vmem_limit_bytes=67_000_000),
        )(*args)

    return jax.shard_map(device_step, mesh=mesh, in_specs=(token_spec,) + (P(),) * 12, out_specs=token_spec, check_vma=False)
```

profile of v0, /device:TPU:21, one launch (start us, length us, event | category | flops | bytes accessed | tf_op | source)
XLA Modules:
  0.0 91.4 jit_solution(15438260987118736532)
XLA Ops:
  0.0 89.1 %shard_map.127 = bf16[32,16,1024]{2,1,0:T(8,128)(2,1)} custom-call(bf16[32,16,1024]{2,1,0:T(8,128)(2,1)} %x_ref.1, f32[2,1024]{1,0:T(2,128)} %g1_hbm.1, f32[2,1024]{1,0:T(2,128)} %s1_hbm.1, bf16[2,3072,1024]{2,1,0:T(8,128)(2,1)} %bitcast.4, f32[2,3,16,64]{3,2,1,0:T(8,128)} %bqkv_hbm.1, bf16[2,1024,1024]{2,1,0:T(8,128)(2,1)} %bitcast.5, f32[2,1024]{1,0:T(2,128)} %bout_hbm.1, ...), custom_call_target="tpu_custom_call" | custom-call | tf_op jit(solution)/shard_map/pallas_call | solution.py:178
  89.1 2.3 %copy.15 = bf16[32,16,1024]{2,1,0:T(8,128)(2,1)} copy(bf16[32,16,1024]{2,1,0:T(8,128)(2,1)} %shard_map.127) | data formatting | bytes 2097152
where the time goes:
time: 91.5 us; the launch traced here: 91.4 us
  Pallas kernels  89.1 us (97%)
  local copies, waits for them, and re-layouts  2.31 us (3%)
    pallas_call x1, Pallas kernels, device_step(): pl.pallas_call(functools.partial(kernel, peers), out_shape=jax.ShapeDtype...  89.1 us
    unnamed x1, local copies, waits for them, and re-layouts  2.31 us

commit v1 on v0

--- a/solution.py
+++ b/solution.py
@@ -62,7 +62,7 @@
 
     order = sorted(range(1, peers), key=lambda s: -min(s // 2, (peers - s) // 2))
     my_rows = pl.ds(pl.multiple_of(me * block, block), block)
-    for image in range(images):
+    def send_in(image):
         for step in order:
             peer = lax.rem(me + step, peers)
             pltpu.make_async_remote_copy(
@@ -70,6 +70,8 @@
                 send_sem=in_send, recv_sem=in_recv.at[image],
                 device_id={'sp': peer}, device_id_type=MESH).start()
         pltpu.make_async_copy(x_ref.at[me * images + image], hid.at[image, my_rows, :], in_recv.at[image]).start()
+
+    send_in(0)
     for layer in range(1, layers):
         for copy in weight_copies(layer):
             copy.start()
@@ -89,6 +91,10 @@
         @pl.when(layer == 0)
         def _():
             pltpu.make_async_copy(state, state, in_recv.at[image]).wait()
+
+            @pl.when(image < images - 1)
+            def _():
+                send_in(image + 1)
 
         row = pl.ds(layer, 1)
         norm_rows(state, normed, g1[row, :], s1[row, :], 32)

time: 91.5 us -> 91.9 us (level)
  no operation moved by 1% of the time
where the time goes in v1:
time: 91.9 us; the launch traced here: 91.8 us
  Pallas kernels  89.5 us (97%)
  local copies, waits for them, and re-layouts  2.31 us (3%)
    pallas_call x1, Pallas kernels, device_step(): pl.pallas_call(functools.partial(kernel, peers), out_shape=jax.ShapeDtype...  89.5 us
    unnamed x1, local copies, waits for them, and re-layouts  2.31 us

profile of v1, /device:TPU:21, one launch (start us, length us, event | category | flops | bytes accessed | tf_op | source)
XLA Modules:
  0.0 91.8 jit_solution(1603586883172274511)
XLA Ops:
  0.0 89.5 %shard_map.127 = bf16[32,16,1024]{2,1,0:T(8,128)(2,1)} custom-call(bf16[32,16,1024]{2,1,0:T(8,128)(2,1)} %x_ref.1, f32[2,1024]{1,0:T(2,128)} %g1_hbm.1, f32[2,1024]{1,0:T(2,128)} %s1_hbm.1, bf16[2,3072,1024]{2,1,0:T(8,128)(2,1)} %bitcast.4, f32[2,3,16,64]{3,2,1,0:T(8,128)} %bqkv_hbm.1, bf16[2,1024,1024]{2,1,0:T(8,128)(2,1)} %bitcast.5, f32[2,1024]{1,0:T(2,128)} %bout_hbm.1, ...), custom_call_target="tpu_custom_call" | custom-call | tf_op jit(solution)/shard_map/pallas_call | solution.py:184
  89.5 2.3 %copy.15 = bf16[32,16,1024]{2,1,0:T(8,128)(2,1)} copy(bf16[32,16,1024]{2,1,0:T(8,128)(2,1)} %shard_map.127) | data formatting | bytes 2097152

commit v2 on v1

--- a/solution.py
+++ b/solution.py
@@ -35,7 +35,7 @@
 def kernel(peers, x_ref, g1_hbm, s1_hbm, wqkv_hbm, bqkv_hbm, wout_hbm, bout_hbm, g2_hbm, s2_hbm, wup_hbm, bup_hbm, wdown_hbm, bdown_hbm,
            out_ref,
            hid, wqkv, wout, wup, wdown, g1, s1, bqkv, bout, g2, s2, bup, bdown,
-           normed, q_t, v_t, keys, mixed, active,
+           normed, q_t, v_t, keys, mixed, active, scores, probs, peaks, totals, mixed_t,
            w_sem, p_sem, in_send, in_recv, out_send, out_recv):
     images = hid.shape[0]
     block = x_ref.shape[1]
@@ -114,19 +114,37 @@
 
         scale = head_dim ** -0.5 / math.log(2.0)
         zeros = jnp.zeros((head_dim, tokens), BF)
-        for pair in range(0, heads, 2):
-            cols = pl.ds(pair * head_dim, 2 * head_dim)
-            outs = []
-            for head in (pair, pair + 1):
-                q_head = q_t[pl.ds(head * head_dim, head_dim), :]
-                rhs = jnp.concatenate([q_head, zeros] if head == pair else [zeros, q_head], axis=0)
-                scores = jnp.dot(keys[:, cols], rhs, preferred_element_type=F32)
-                peak = jnp.max(scores, axis=0, keepdims=True)
-                prob = jnp.exp2((scores - peak) * scale)
-                total = jnp.sum(prob, axis=0, keepdims=True)
-                mix = jnp.dot(v_t[pl.ds(head * head_dim, head_dim), :], prob.astype(BF), preferred_element_type=F32)
-                outs.append(mix * (1.0 / total))
-            mixed[:, cols] = jnp.concatenate(outs, axis=0).T.astype(BF)
+
+        def score(head):
+            pair = head // 2 * 2
+            q_head = q_t[pl.ds(head * head_dim, head_dim), :]
+            rhs = jnp.concatenate([q_head, zeros] if head == pair else [zeros, q_head], axis=0)
+            part = jnp.dot(keys[:, pl.ds(pair * head_dim, 2 * head_dim)], rhs, preferred_element_type=F32)
+            scores[head % 4] = part
+            peaks[head % 4] = jnp.max(part, axis=0, keepdims=True)
+
+        def soften(head):
+            prob = jnp.exp2((scores[head % 4] - peaks[head % 4]) * scale)
+            totals[head % 4] = jnp.sum(prob, axis=0, keepdims=True)
+            probs[head % 4] = prob.astype(BF)
+
+        def mix(head):
+            part = jnp.dot(v_t[pl.ds(head * head_dim, head_dim), :], probs[head % 4], preferred_element_type=F32)
+            mixed_t[pl.ds(head * head_dim, head_dim), :] = part * (1.0 / totals[head % 4])
+
+        for step in range(0, heads + 4, 2):
+            for head in (step, step + 1):
+                if head < heads:
+                    score(head)
+            for head in (step - 2, step - 1):
+                if 0 <= head < heads:
+                    soften(head)
+            for head in (step - 4, step - 3):
+                if 0 <= head < heads:
+                    mix(head)
+            if step >= 4:
+                cols = pl.ds((step - 4) * head_dim, 2 * head_dim)
+                mixed[:, cols] = mixed_t[cols, :].T.astype(BF)
 
         weight_wait(1)
         for start in range(0, width, 512):
@@ -196,6 +214,11 @@
                 pltpu.VMEM((tokens, inner), BF),
                 pltpu.VMEM((tokens, inner), BF),
                 pltpu.VMEM((tokens, mlp_dim), BF),
+                pltpu.VMEM((4, tokens, tokens), F32),
+                pltpu.VMEM((4, tokens, tokens), BF),
+                pltpu.VMEM((4, 1, tokens), F32),
+                pltpu.VMEM((4, 1, tokens), F32),
+                pltpu.VMEM((inner, tokens), F32),
                 pltpu.SemaphoreType.DMA((layers, 4)),
                 pltpu.SemaphoreType.DMA((8,)),
                 pltpu.SemaphoreType.DMA,

time: 91.9 us -> 81 us (0.88)
  Pallas kernels: 89.5 us -> 78.6 us
    pallas_call x1, Pallas kernels: 89.5 us -> 78.6 us  [device_step(): pl.pallas_call(functools.partial(kernel, peers), out_shape=jax.ShapeDtype...]
where the time goes in v2:
time: 81 us; the launch traced here: 80.9 us
  Pallas kernels  78.6 us (97%)
  local copies, waits for them, and re-layouts  2.31 us (3%)
    pallas_call x1, Pallas kernels, device_step(): pl.pallas_call(functools.partial(kernel, peers), out_shape=jax.ShapeDtype...  78.6 us
    unnamed x1, local copies, waits for them, and re-layouts  2.31 us

profile of v2, /device:TPU:21, one launch (start us, length us, event | category | flops | bytes accessed | tf_op | source)
XLA Modules:
  0.0 80.9 jit_solution(16910679055129455540)
XLA Ops:
  0.0 78.6 %shard_map.127 = bf16[32,16,1024]{2,1,0:T(8,128)(2,1)} custom-call(bf16[32,16,1024]{2,1,0:T(8,128)(2,1)} %x_ref.1, f32[2,1024]{1,0:T(2,128)} %g1_hbm.1, f32[2,1024]{1,0:T(2,128)} %s1_hbm.1, bf16[2,3072,1024]{2,1,0:T(8,128)(2,1)} %bitcast.4, f32[2,3,16,64]{3,2,1,0:T(8,128)} %bqkv_hbm.1, bf16[2,1024,1024]{2,1,0:T(8,128)(2,1)} %bitcast.5, f32[2,1024]{1,0:T(2,128)} %bout_hbm.1, ...), custom_call_target="tpu_custom_call" | custom-call | tf_op jit(solution)/shard_map/pallas_call | solution.py:202
  78.6 2.3 %copy.15 = bf16[32,16,1024]{2,1,0:T(8,128)(2,1)} copy(bf16[32,16,1024]{2,1,0:T(8,128)(2,1)} %shard_map.127) | data formatting | bytes 2097152

commit v3 on v2

--- a/solution.py
+++ b/solution.py
@@ -83,10 +83,10 @@
         layer = lax.rem(step_idx, layers)
         state = hid.at[image]
 
-        def weight_wait(i):
-            @pl.when(image == 0)
-            def _():
-                weight_copies(layer)[i].wait()
+        @pl.when(image == 0)
+        def _():
+            for copy in weight_copies(layer):
+                copy.wait()
 
         @pl.when(layer == 0)
         def _():
@@ -98,7 +98,6 @@
 
         row = pl.ds(layer, 1)
         norm_rows(state, normed, g1[row, :], s1[row, :], 32)
-        weight_wait(0)
 
         for slot, dst in ((0, q_t), (2, v_t)):
             bias = bqkv[layer, slot].T
@@ -146,19 +145,16 @@
                 cols = pl.ds((step - 4) * head_dim, 2 * head_dim)
                 mixed[:, cols] = mixed_t[cols, :].T.astype(BF)
 
-        weight_wait(1)
         for start in range(0, width, 512):
             cols = pl.ds(start, 512)
             part = jnp.dot(mixed[...], wout[layer, :, cols], preferred_element_type=F32) + bout[row, cols]
             state[:, cols] = (state[:, cols].astype(F32) + part).astype(BF)
 
         norm_rows(state, normed, g2[row, :], s2[row, :], 32)
-        weight_wait(2)
         for start in range(0, mlp_dim, 512):
             cols = pl.ds(start, 512)
             part = jnp.dot(normed[...], wup[layer, :, cols], preferred_element_type=F32) + bup[row, cols]
             active[:, cols] = gelu(part).astype(BF)
-        weight_wait(3)
         for start in range(0, width, 512):
             cols = pl.ds(start, 512)
             part = jnp.dot(active[...], wdown[layer, :, cols], preferred_element_type=F32) + bdown[row, cols]

time: 81 us -> 77 us (0.951)
  Pallas kernels: 78.6 us -> 74.6 us
    pallas_call x1, Pallas kernels: 78.6 us -> 74.6 us  [device_step(): pl.pallas_call(functools.partial(kernel, peers), out_shape=jax.ShapeDtype...]
where the time goes in v3:
time: 77 us; the launch traced here: 76.9 us
  Pallas kernels  74.6 us (97%)
  local copies, waits for them, and re-layouts  2.31 us (3%)
    pallas_call x1, Pallas kernels, device_step(): pl.pallas_call(functools.partial(kernel, peers), out_shape=jax.ShapeDtype...  74.6 us
    unnamed x1, local copies, waits for them, and re-layouts  2.31 us

profile of v3, /device:TPU:21, one launch (start us, length us, event | category | flops | bytes accessed | tf_op | source)
XLA Modules:
  0.0 76.9 jit_solution(14436050134651104905)
XLA Ops:
  0.0 74.6 %shard_map.127 = bf16[32,16,1024]{2,1,0:T(8,128)(2,1)} custom-call(bf16[32,16,1024]{2,1,0:T(8,128)(2,1)} %x_ref.1, f32[2,1024]{1,0:T(2,128)} %g1_hbm.1, f32[2,1024]{1,0:T(2,128)} %s1_hbm.1, bf16[2,3072,1024]{2,1,0:T(8,128)(2,1)} %bitcast.4, f32[2,3,16,64]{3,2,1,0:T(8,128)} %bqkv_hbm.1, bf16[2,1024,1024]{2,1,0:T(8,128)(2,1)} %bitcast.5, f32[2,1024]{1,0:T(2,128)} %bout_hbm.1, ...), custom_call_target="tpu_custom_call" | custom-call | tf_op jit(solution)/shard_map/pallas_call | solution.py:198
  74.6 2.3 %copy.15 = bf16[32,16,1024]{2,1,0:T(8,128)(2,1)} copy(bf16[32,16,1024]{2,1,0:T(8,128)(2,1)} %shard_map.127) | data formatting | bytes 2097152

commit v4 on v3

--- a/solution.py
+++ b/solution.py
@@ -36,7 +36,7 @@
            out_ref,
            hid, wqkv, wout, wup, wdown, g1, s1, bqkv, bout, g2, s2, bup, bdown,
            normed, q_t, v_t, keys, mixed, active, scores, probs, peaks, totals, mixed_t,
-           w_sem, p_sem, in_send, in_recv, out_send, out_recv):
+           ready, w_sem, p_sem, in_send, in_recv, out_send, out_recv):
     images = hid.shape[0]
     block = x_ref.shape[1]
     layers, heads, head_dim = bqkv.shape[0], bqkv.shape[2], bqkv.shape[3]
@@ -51,27 +51,53 @@
         return [pltpu.make_async_copy(src.at[layer], dst.at[layer], w_sem.at[layer, i]) for i, (src, dst) in enumerate((
             (wqkv_hbm, wqkv), (wout_hbm, wout), (wup_hbm, wup), (wdown_hbm, wdown)))]
 
+    my_rows = pl.ds(pl.multiple_of(me * block, block), block)
+
+    def send_in(image, peer):
+        pltpu.make_async_remote_copy(
+            src_ref=x_ref.at[peer * images + image], dst_ref=hid.at[image, my_rows, :],
+            send_sem=in_send, recv_sem=in_recv.at[image],
+            device_id={'sp': peer}, device_id_type=MESH).start()
+
     barrier = pltpu.get_barrier_semaphore()
-    for step in range(1, peers):
-        pl.semaphore_signal(barrier, inc=1, device_id={'sp': lax.rem(me + step, peers)}, device_id_type=MESH)
+
+    @pl.loop(me + 1, peers)
+    def _(peer):
+        pl.semaphore_signal(barrier, inc=1, device_id={'sp': peer}, device_id_type=MESH)
+
+    @pl.when(me > 0)
+    def _():
+        pl.semaphore_wait(barrier, me)
+
+    @pl.loop(0, me)
+    def _(peer):
+        pl.semaphore_signal(ready.at[me], inc=1, device_id={'sp': peer}, device_id_type=MESH)
+
+    @pl.loop(0, me)
+    def _(peer):
+        send_in(0, peer)
+
     for copy in params:
         copy.start()
     for copy in weight_copies(0):
         copy.start()
-    pl.semaphore_wait(barrier, peers - 1)
-
-    order = sorted(range(1, peers), key=lambda s: -min(s // 2, (peers - s) // 2))
-    my_rows = pl.ds(pl.multiple_of(me * block, block), block)
-    def send_in(image):
-        for step in order:
-            peer = lax.rem(me + step, peers)
-            pltpu.make_async_remote_copy(
-                src_ref=x_ref.at[peer * images + image], dst_ref=hid.at[image, my_rows, :],
-                send_sem=in_send, recv_sem=in_recv.at[image],
-                device_id={'sp': peer}, device_id_type=MESH).start()
+
+    @pl.loop(me + 1, peers)
+    def _(peer):
+        pl.semaphore_wait(ready.at[peer], 1)
+        send_in(0, peer)
+
+    for image in range(images):
         pltpu.make_async_copy(x_ref.at[me * images + image], hid.at[image, my_rows, :], in_recv.at[image]).start()
-
-    send_in(0)
+    for image in range(1, images):
+        @pl.loop(0, me)
+        def _(peer):
+            send_in(image, peer)
+
+        @pl.loop(me + 1, peers)
+        def _(peer):
+            send_in(image, peer)
+
     for layer in range(1, layers):
         for copy in weight_copies(layer):
             copy.start()
@@ -91,10 +117,6 @@
         @pl.when(layer == 0)
         def _():
             pltpu.make_async_copy(state, state, in_recv.at[image]).wait()
-
-            @pl.when(image < images - 1)
-            def _():
-                send_in(image + 1)
 
         row = pl.ds(layer, 1)
         norm_rows(state, normed, g1[row, :], s1[row, :], 32)
@@ -162,13 +184,15 @@
 
         @pl.when(layer == layers - 1)
         def _():
-            for step in order:
+            @pl.loop(1, peers)
+            def _(step):
                 peer = lax.rem(me + step, peers)
                 pltpu.make_async_remote_copy(
                     src_ref=hid.at[image, pl.ds(pl.multiple_of(peer * block, block), block), :],
                     dst_ref=out_ref.at[me * images + image],
                     send_sem=out_send, recv_sem=out_recv,
                     device_id={'sp': peer}, device_id_type=MESH).start()
+
             pltpu.make_async_copy(hid.at[image, my_rows, :], out_ref.at[me * images + image], out_recv).start()
         return carry
 
@@ -215,6 +239,7 @@
                 pltpu.VMEM((4, 1, tokens), F32),
                 pltpu.VMEM((4, 1, tokens), F32),
                 pltpu.VMEM((inner, tokens), F32),
+                pltpu.SemaphoreType.REGULAR((peers,)),
                 pltpu.SemaphoreType.DMA((layers, 4)),
                 pltpu.SemaphoreType.DMA((8,)),
                 pltpu.SemaphoreType.DMA,

time: 77 us -> 77.5 us (level)
  no operation moved by 1% of the time
where the time goes in v4:
time: 77.5 us; the launch traced here: 76.7 us
  Pallas kernels  74.4 us (96%)
  local copies, waits for them, and re-layouts  2.31 us (3%)
    pallas_call x1, Pallas kernels, device_step(): pl.pallas_call(functools.partial(kernel, peers), out_shape=jax.ShapeDtype...  74.4 us
    unnamed x1, local copies, waits for them, and re-layouts  2.31 us

profile of v4, /device:TPU:21, one launch (start us, length us, event | category | flops | bytes accessed | tf_op | source)
XLA Modules:
  0.0 76.7 jit_solution(10646843931441346371)
XLA Ops:
  0.0 74.4 %shard_map.127 = bf16[32,16,1024]{2,1,0:T(8,128)(2,1)} custom-call(bf16[32,16,1024]{2,1,0:T(8,128)(2,1)} %x_ref.1, f32[2,1024]{1,0:T(2,128)} %g1_hbm.1, f32[2,1024]{1,0:T(2,128)} %s1_hbm.1, bf16[2,3072,1024]{2,1,0:T(8,128)(2,1)} %bitcast.4, f32[2,3,16,64]{3,2,1,0:T(8,128)} %bqkv_hbm.1, bf16[2,1024,1024]{2,1,0:T(8,128)(2,1)} %bitcast.5, f32[2,1024]{1,0:T(2,128)} %bout_hbm.1, ...), custom_call_target="tpu_custom_call" | custom-call | tf_op jit(solution)/shard_map/pallas_call | solution.py:222
  74.4 2.3 %copy.15 = bf16[32,16,1024]{2,1,0:T(8,128)(2,1)} copy(bf16[32,16,1024]{2,1,0:T(8,128)(2,1)} %shard_map.127) | data formatting | bytes 2097152

commit v5 on v4

--- a/solution.py
+++ b/solution.py
@@ -73,9 +73,12 @@
     def _(peer):
         pl.semaphore_signal(ready.at[me], inc=1, device_id={'sp': peer}, device_id_type=MESH)
 
-    @pl.loop(0, me)
-    def _(peer):
-        send_in(0, peer)
+    for core in range(2):
+        @pl.loop(0, me)
+        def _(peer):
+            @pl.when(lax.rem(peer, 2) == core)
+            def _():
+                send_in(0, peer)
 
     for copy in params:
         copy.start()
@@ -87,17 +90,7 @@
         pl.semaphore_wait(ready.at[peer], 1)
         send_in(0, peer)
 
-    for image in range(images):
-        pltpu.make_async_copy(x_ref.at[me * images + image], hid.at[image, my_rows, :], in_recv.at[image]).start()
-    for image in range(1, images):
-        @pl.loop(0, me)
-        def _(peer):
-            send_in(image, peer)
-
-        @pl.loop(me + 1, peers)
-        def _(peer):
-            send_in(image, peer)
-
+    pltpu.make_async_copy(x_ref.at[me * images], hid.at[0, my_rows, :], in_recv.at[0]).start()
     for layer in range(1, layers):
         for copy in weight_copies(layer):
             copy.start()
@@ -117,6 +110,14 @@
         @pl.when(layer == 0)
         def _():
             pltpu.make_async_copy(state, state, in_recv.at[image]).wait()
+
+            @pl.when(image < images - 1)
+            def _():
+                pltpu.make_async_copy(x_ref.at[me * images + image + 1], hid.at[image + 1, my_rows, :], in_recv.at[image + 1]).start()
+
+                @pl.loop(1, peers)
+                def _(step):
+                    send_in(image + 1, lax.rem(me + step, peers))
 
         row = pl.ds(layer, 1)
         norm_rows(state, normed, g1[row, :], s1[row, :], 32)
@@ -172,28 +173,55 @@
             part = jnp.dot(mixed[...], wout[layer, :, cols], preferred_element_type=F32) + bout[row, cols]
             state[:, cols] = (state[:, cols].astype(F32) + part).astype(BF)
 
-        norm_rows(state, normed, g2[row, :], s2[row, :], 32)
-        for start in range(0, mlp_dim, 512):
-            cols = pl.ds(start, 512)
-            part = jnp.dot(normed[...], wup[layer, :, cols], preferred_element_type=F32) + bup[row, cols]
-            active[:, cols] = gelu(part).astype(BF)
-        for start in range(0, width, 512):
-            cols = pl.ds(start, 512)
-            part = jnp.dot(active[...], wdown[layer, :, cols], preferred_element_type=F32) + bdown[row, cols]
-            state[:, cols] = (state[:, cols].astype(F32) + part).astype(BF)
-
-        @pl.when(layer == layers - 1)
-        def _():
-            @pl.loop(1, peers)
-            def _(step):
-                peer = lax.rem(me + step, peers)
-                pltpu.make_async_remote_copy(
-                    src_ref=hid.at[image, pl.ds(pl.multiple_of(peer * block, block), block), :],
-                    dst_ref=out_ref.at[me * images + image],
-                    send_sem=out_send, recv_sem=out_recv,
-                    device_id={'sp': peer}, device_id_type=MESH).start()
-
-            pltpu.make_async_copy(hid.at[image, my_rows, :], out_ref.at[me * images + image], out_recv).start()
+        half = tokens // 2
+
+        def norm_two(first):
+            norm_rows(state.at[pl.ds(first, half), :], normed.at[pl.ds(first, half), :], g2[row, :], s2[row, :], 32)
+
+        def widen(first):
+            rows = pl.ds(first, half)
+            for start in range(0, mlp_dim, 512):
+                cols = pl.ds(start, 512)
+                part = jnp.dot(normed[rows, :], wup[layer, :, cols], preferred_element_type=F32) + bup[row, cols]
+                active[rows, cols] = gelu(part).astype(BF)
+
+        def narrow(first):
+            rows = pl.ds(first, half)
+            for start in range(0, width, 512):
+                cols = pl.ds(start, 512)
+                part = jnp.dot(active[rows, :], wdown[layer, :, cols], preferred_element_type=F32) + bdown[row, cols]
+                state[rows, cols] = (state[rows, cols].astype(F32) + part).astype(BF)
+
+        def send_out(first):
+            @pl.when(layer == layers - 1)
+            def _():
+                low = first // block
+                high = low + half // block
+                slot = me * images + image
+
+                @pl.loop(low, high)
+                def _(peer):
+                    rows = pl.ds(pl.multiple_of(peer * block, block), block)
+
+                    @pl.when(peer != me)
+                    def _():
+                        pltpu.make_async_remote_copy(
+                            src_ref=hid.at[image, rows, :], dst_ref=out_ref.at[slot],
+                            send_sem=out_send, recv_sem=out_recv,
+                            device_id={'sp': peer}, device_id_type=MESH).start()
+
+                    @pl.when(peer == me)
+                    def _():
+                        out_ref[slot] = hid[image, rows, :]
+
+        norm_two(0)
+        widen(0)
+        norm_two(half)
+        narrow(0)
+        send_out(0)
+        widen(half)
+        narrow(half)
+        send_out(half)
         return carry
 
     lax.fori_loop(0, images * layers, body, 0)
@@ -201,7 +229,7 @@
     sent = x_ref.at[pl.ds(0, (peers - 1) * images)]
     pltpu.make_async_copy(sent, sent, in_send).wait()
     pltpu.make_async_copy(sent, sent, out_send).wait()
-    pltpu.make_async_copy(out_ref, out_ref, out_recv).wait()
+    pltpu.make_async_copy(sent, sent, out_recv).wait()
 
 
 def solution(mesh):
@@ -221,9 +249,9 @@
         small = lambda a: pltpu.VMEM(a.shape, a.dtype)
         return pl.pallas_call(
             functools.partial(kernel, peers),
-            out_shape=jax.ShapeDtypeStruct(image_tokens.shape, image_tokens.dtype),
+            out_shape=pltpu.VMEM(image_tokens.shape, image_tokens.dtype),
             in_specs=[pl.BlockSpec(memory_space=pl.ANY)] * len(args),
-            out_specs=pl.BlockSpec(memory_space=pl.ANY),
+            out_specs=pl.BlockSpec(memory_space=pltpu.VMEM),
             scratch_shapes=[
                 pltpu.VMEM((images, tokens, width), BF),
                 small(w_qkv_t), small(w_out_m), small(w_up), small(w_down),
@@ -247,7 +275,7 @@
                 pltpu.SemaphoreType.DMA,
                 pltpu.SemaphoreType.DMA,
             ],
-            compiler_params=pltpu.CompilerParams(collective_id=0, has_side_effects=True, vmem_limit_bytes=67_000_000),
+            compiler_params=pltpu.CompilerParams(collective_id=0, has_side_effects=True, vmem_limit_bytes=65_500_000),
         )(*args)
 
     return jax.shard_map(device_step, mesh=mesh, in_specs=(token_spec,) + (P(),) * 12, out_specs=token_spec, check_vma=False)

time: 77.5 us -> 78.5 us (1.013)
  Pallas kernels: 74.4 us -> 76.7 us
  local copies, waits for them, and re-layouts: 2.31 us -> 0.97 us
    pallas_call x1, Pallas kernels: 74.4 us -> 76.7 us  [device_step(): pl.pallas_call(functools.partial(kernel, peers), out_shape=pltpu.VMEM(ima...]
    unnamed x1, local copies, waits for them, and re-layouts: 2.31 us -> 0.97 us
where the time goes in v5:
time: 78.5 us; the launch traced here: 77.7 us
  Pallas kernels  76.7 us (98%)
  local copies, waits for them, and re-layouts  0.97 us (1%)
    pallas_call x1, Pallas kernels, device_step(): pl.pallas_call(functools.partial(kernel, peers), out_shape=pltpu.VMEM(ima...  76.7 us

profile of v5, /device:TPU:21, one launch (start us, length us, event | category | flops | bytes accessed | tf_op | source)
XLA Modules:
  0.0 77.7 jit_solution(10314964321081940116)
XLA Ops:
  0.0 76.7 %shard_map.127 = bf16[32,16,1024]{2,1,0:T(8,128)(2,1)S(1)} custom-call(bf16[32,16,1024]{2,1,0:T(8,128)(2,1)} %x_ref.1, f32[2,1024]{1,0:T(2,128)} %g1_hbm.1, f32[2,1024]{1,0:T(2,128)} %s1_hbm.1, bf16[2,3072,1024]{2,1,0:T(8,128)(2,1)} %bitcast.4, f32[2,3,16,64]{3,2,1,0:T(8,128)} %bqkv_hbm.1, bf16[2,1024,1024]{2,1,0:T(8,128)(2,1)} %bitcast.5, ...), custom_call_target="tpu_custom_call" | custom-call | tf_op jit(solution)/shard_map/pallas_call | solution.py:250
  76.7 1.0 %copy.15 = bf16[32,16,1024]{2,1,0:T(8,128)(2,1)} copy(bf16[32,16,1024]{2,1,0:T(8,128)(2,1)S(1)} %shard_map.127) | data formatting | bytes 2097152

commit v6 on v4

--- a/solution.py
+++ b/solution.py
@@ -53,51 +53,47 @@
 
     my_rows = pl.ds(pl.multiple_of(me * block, block), block)
 
-    def send_in(image, peer):
-        pltpu.make_async_remote_copy(
-            src_ref=x_ref.at[peer * images + image], dst_ref=hid.at[image, my_rows, :],
-            send_sem=in_send, recv_sem=in_recv.at[image],
-            device_id={'sp': peer}, device_id_type=MESH).start()
-
-    barrier = pltpu.get_barrier_semaphore()
-
-    @pl.loop(me + 1, peers)
-    def _(peer):
-        pl.semaphore_signal(barrier, inc=1, device_id={'sp': peer}, device_id_type=MESH)
-
-    @pl.when(me > 0)
-    def _():
-        pl.semaphore_wait(barrier, me)
-
-    @pl.loop(0, me)
-    def _(peer):
-        pl.semaphore_signal(ready.at[me], inc=1, device_id={'sp': peer}, device_id_type=MESH)
-
-    @pl.loop(0, me)
-    def _(peer):
-        send_in(0, peer)
+    def send_in(image, ask):
+        chips = peers // 2
+        for core in range(2):
+            for parity in range(2):
+                @pl.loop(0, chips // 2)
+                def _(turn):
+                    peer = 4 * lax.rem(me // 4 + turn, chips // 2) + 2 * parity + core
+
+                    if ask:
+                        @pl.when(peer > me)
+                        def _():
+                            pl.semaphore_wait(ready.at[peer], 1)
+
+                    @pl.when(peer != me)
+                    def _():
+                        pltpu.make_async_remote_copy(
+                            src_ref=x_ref.at[peer * images + image], dst_ref=hid.at[image, my_rows, :],
+                            send_sem=in_send, recv_sem=in_recv.at[image],
+                            device_id={'sp': peer}, device_id_type=MESH).start()
+        pltpu.make_async_copy(x_ref.at[me * images + image], hid.at[image, my_rows, :], in_recv.at[image]).start()
 
     for copy in params:
         copy.start()
     for copy in weight_copies(0):
         copy.start()
 
+    barrier = pltpu.get_barrier_semaphore()
+
     @pl.loop(me + 1, peers)
     def _(peer):
-        pl.semaphore_wait(ready.at[peer], 1)
-        send_in(0, peer)
-
-    for image in range(images):
-        pltpu.make_async_copy(x_ref.at[me * images + image], hid.at[image, my_rows, :], in_recv.at[image]).start()
-    for image in range(1, images):
-        @pl.loop(0, me)
-        def _(peer):
-            send_in(image, peer)
-
-        @pl.loop(me + 1, peers)
-        def _(peer):
-            send_in(image, peer)
-
+        pl.semaphore_signal(barrier, inc=1, device_id={'sp': peer}, device_id_type=MESH)
+
+    @pl.when(me > 0)
+    def _():
+        pl.semaphore_wait(barrier, me)
+
+    @pl.loop(0, me)
+    def _(peer):
+        pl.semaphore_signal(ready.at[me], inc=1, device_id={'sp': peer}, device_id_type=MESH)
+
+    send_in(0, True)
     for layer in range(1, layers):
         for copy in weight_copies(layer):
             copy.start()
@@ -172,6 +168,11 @@
             part = jnp.dot(mixed[...], wout[layer, :, cols], preferred_element_type=F32) + bout[row, cols]
             state[:, cols] = (state[:, cols].astype(F32) + part).astype(BF)
 
+        @pl.when(step_idx == 0)
+        def _():
+            for other in range(1, images):
+                send_in(other, False)
+
         norm_rows(state, normed, g2[row, :], s2[row, :], 32)
         for start in range(0, mlp_dim, 512):
             cols = pl.ds(start, 512)
@@ -184,16 +185,23 @@
 
         @pl.when(layer == layers - 1)
         def _():
-            @pl.loop(1, peers)
-            def _(step):
-                peer = lax.rem(me + step, peers)
-                pltpu.make_async_remote_copy(
-                    src_ref=hid.at[image, pl.ds(pl.multiple_of(peer * block, block), block), :],
-                    dst_ref=out_ref.at[me * images + image],
-                    send_sem=out_send, recv_sem=out_recv,
-                    device_id={'sp': peer}, device_id_type=MESH).start()
-
-            pltpu.make_async_copy(hid.at[image, my_rows, :], out_ref.at[me * images + image], out_recv).start()
+            slot = me * images + image
+
+            @pl.loop(0, peers)
+            def _(peer):
+                rows = pl.ds(pl.multiple_of(peer * block, block), block)
+
+                @pl.when(peer != me)
+                def _():
+                    pltpu.make_async_remote_copy(
+                        src_ref=hid.at[image, rows, :], dst_ref=out_ref.at[slot],
+                        send_sem=out_send, recv_sem=out_recv,
+                        device_id={'sp': peer}, device_id_type=MESH).start()
+
+                @pl.when(peer == me)
+                def _():
+                    out_ref[slot] = hid[image, rows, :]
+
         return carry
 
     lax.fori_loop(0, images * layers, body, 0)
@@ -201,7 +209,7 @@
     sent = x_ref.at[pl.ds(0, (peers - 1) * images)]
     pltpu.make_async_copy(sent, sent, in_send).wait()
     pltpu.make_async_copy(sent, sent, out_send).wait()
-    pltpu.make_async_copy(out_ref, out_ref, out_recv).wait()
+    pltpu.make_async_copy(sent, sent, out_recv).wait()
 
 
 def solution(mesh):
@@ -221,9 +229,9 @@
         small = lambda a: pltpu.VMEM(a.shape, a.dtype)
         return pl.pallas_call(
             functools.partial(kernel, peers),
-            out_shape=jax.ShapeDtypeStruct(image_tokens.shape, image_tokens.dtype),
+            out_shape=pltpu.VMEM(image_tokens.shape, image_tokens.dtype),
             in_specs=[pl.BlockSpec(memory_space=pl.ANY)] * len(args),
-            out_specs=pl.BlockSpec(memory_space=pl.ANY),
+            out_specs=pl.BlockSpec(memory_space=pltpu.VMEM),
             scratch_shapes=[
                 pltpu.VMEM((images, tokens, width), BF),
                 small(w_qkv_t), small(w_out_m), small(w_up), small(w_down),
@@ -247,7 +255,7 @@
                 pltpu.SemaphoreType.DMA,
                 pltpu.SemaphoreType.DMA,
             ],
-            compiler_params=pltpu.CompilerParams(collective_id=0, has_side_effects=True, vmem_limit_bytes=67_000_000),
+            compiler_params=pltpu.CompilerParams(collective_id=0, has_side_effects=True, vmem_limit_bytes=65_500_000),
         )(*args)
 
     return jax.shard_map(device_step, mesh=mesh, in_specs=(token_spec,) + (P(),) * 12, out_specs=token_spec, check_vma=False)

time: 77.5 us -> 73.3 us (0.946)
  Pallas kernels: 74.4 us -> 71.8 us
  local copies, waits for them, and re-layouts: 2.31 us -> 0.97 us
    pallas_call x1, Pallas kernels: 74.4 us -> 71.8 us  [device_step(): pl.pallas_call(functools.partial(kernel, peers), out_shape=pltpu.VMEM(ima...]
    unnamed x1, local copies, waits for them, and re-layouts: 2.31 us -> 0.97 us
where the time goes in v6:
time: 73.3 us; the launch traced here: 72.8 us
  Pallas kernels  71.8 us (98%)
  local copies, waits for them, and re-layouts  0.97 us (1%)
    pallas_call x1, Pallas kernels, device_step(): pl.pallas_call(functools.partial(kernel, peers), out_shape=pltpu.VMEM(ima...  71.8 us

profile of v6, /device:TPU:21, one launch (start us, length us, event | category | flops | bytes accessed | tf_op | source)
XLA Modules:
  0.0 72.8 jit_solution(9790428845681775437)
XLA Ops:
  0.0 71.8 %shard_map.127 = bf16[32,16,1024]{2,1,0:T(8,128)(2,1)S(1)} custom-call(bf16[32,16,1024]{2,1,0:T(8,128)(2,1)} %x_ref.1, f32[2,1024]{1,0:T(2,128)} %g1_hbm.1, f32[2,1024]{1,0:T(2,128)} %s1_hbm.1, bf16[2,3072,1024]{2,1,0:T(8,128)(2,1)} %bitcast.4, f32[2,3,16,64]{3,2,1,0:T(8,128)} %bqkv_hbm.1, bf16[2,1024,1024]{2,1,0:T(8,128)(2,1)} %bitcast.5, ...), custom_call_target="tpu_custom_call" | custom-call | tf_op jit(solution)/shard_map/pallas_call | solution.py:230
  71.8 1.0 %copy.15 = bf16[32,16,1024]{2,1,0:T(8,128)(2,1)} copy(bf16[32,16,1024]{2,1,0:T(8,128)(2,1)S(1)} %shard_map.127) | data formatting | bytes 2097152

commit v7 on v6

--- a/solution.py
+++ b/solution.py
@@ -30,6 +30,11 @@
     c0 = math.sqrt(2.0 / math.pi)
     c1 = c0 * 0.044715
     return 0.5 * x * (1.0 + jnp.tanh(x * (c0 + c1 * (x * x))))
+
+
+def hops(peers, parity):
+    chips = peers // 2
+    return sorted(range(parity, chips, 2), key=lambda hop: (-min(hop, chips - hop), hop))
 
 
 def kernel(peers, x_ref, g1_hbm, s1_hbm, wqkv_hbm, bqkv_hbm, wout_hbm, bout_hbm, g2_hbm, s2_hbm, wup_hbm, bup_hbm, wdown_hbm, bdown_hbm,
@@ -54,12 +59,11 @@
     my_rows = pl.ds(pl.multiple_of(me * block, block), block)
 
     def send_in(image, ask):
-        chips = peers // 2
         for core in range(2):
             for parity in range(2):
-                @pl.loop(0, chips // 2)
-                def _(turn):
-                    peer = 4 * lax.rem(me // 4 + turn, chips // 2) + 2 * parity + core
+                odd = lax.rem(me // 2 + parity, 2)
+                for even_hop, odd_hop in zip(hops(peers, 0), hops(peers, 1)):
+                    peer = 2 * lax.rem(me // 2 + even_hop + odd * (odd_hop - even_hop), peers // 2) + core
 
                     if ask:
                         @pl.when(peer > me)
@@ -107,7 +111,7 @@
 
         @pl.when(image == 0)
         def _():
-            for copy in weight_copies(layer):
+            for copy in weight_copies(layer)[:2]:
                 copy.wait()
 
         @pl.when(layer == 0)
@@ -168,6 +172,11 @@
             part = jnp.dot(mixed[...], wout[layer, :, cols], preferred_element_type=F32) + bout[row, cols]
             state[:, cols] = (state[:, cols].astype(F32) + part).astype(BF)
 
+        @pl.when(image == 0)
+        def _():
+            for copy in weight_copies(layer)[2:]:
+                copy.wait()
+
         @pl.when(step_idx == 0)
         def _():
             for other in range(1, images):
@@ -187,20 +196,19 @@
         def _():
             slot = me * images + image
 
-            @pl.loop(0, peers)
-            def _(peer):
-                rows = pl.ds(pl.multiple_of(peer * block, block), block)
-
-                @pl.when(peer != me)
-                def _():
-                    pltpu.make_async_remote_copy(
-                        src_ref=hid.at[image, rows, :], dst_ref=out_ref.at[slot],
-                        send_sem=out_send, recv_sem=out_recv,
-                        device_id={'sp': peer}, device_id_type=MESH).start()
-
-                @pl.when(peer == me)
-                def _():
-                    out_ref[slot] = hid[image, rows, :]
+            for hop in sorted(hops(peers, 0) + hops(peers, 1), key=lambda hop: (-min(hop, peers // 2 - hop), hop)):
+                for core in range(2):
+                    peer = 2 * lax.rem(me // 2 + hop, peers // 2) + core
+                    rows = pl.ds(pl.multiple_of(peer * block, block), block)
+
+                    @pl.when(peer != me)
+                    def _():
+                        pltpu.make_async_remote_copy(
+                            src_ref=hid.at[image, rows, :], dst_ref=out_ref.at[slot],
+                            send_sem=out_send, recv_sem=out_recv,
+                            device_id={'sp': peer}, device_id_type=MESH).start()
+
+            out_ref[slot] = hid[image, my_rows, :]
 
         return carry
 

time: 73.3 us -> 75 us (1.023)
  Pallas kernels: 71.8 us -> 74 us
    pallas_call x1, Pallas kernels: 71.8 us -> 74 us  [device_step(): pl.pallas_call(functools.partial(kernel, peers), out_shape=pltpu.VMEM(ima...]
where the time goes in v7:
time: 75 us
  Pallas kernels  74 us (99%)
  local copies, waits for them, and re-layouts  0.97 us (1%)
    pallas_call x1, Pallas kernels, device_step(): pl.pallas_call(functools.partial(kernel, peers), out_shape=pltpu.VMEM(ima...  74 us

profile of v7, /device:TPU:21, one launch (start us, length us, event | category | flops | bytes accessed | tf_op | source)
XLA Modules:
  0.0 75.0 jit_solution(7499367310873546099)
XLA Ops:
  0.0 74.0 %shard_map.127 = bf16[32,16,1024]{2,1,0:T(8,128)(2,1)S(1)} custom-call(bf16[32,16,1024]{2,1,0:T(8,128)(2,1)} %x_ref.1, f32[2,1024]{1,0:T(2,128)} %g1_hbm.1, f32[2,1024]{1,0:T(2,128)} %s1_hbm.1, bf16[2,3072,1024]{2,1,0:T(8,128)(2,1)} %bitcast.4, f32[2,3,16,64]{3,2,1,0:T(8,128)} %bqkv_hbm.1, bf16[2,1024,1024]{2,1,0:T(8,128)(2,1)} %bitcast.5, ...), custom_call_target="tpu_custom_call" | custom-call | tf_op jit(solution)/shard_map/pallas_call | solution.py:238
  74.0 1.0 %copy.15 = bf16[32,16,1024]{2,1,0:T(8,128)(2,1)} copy(bf16[32,16,1024]{2,1,0:T(8,128)(2,1)S(1)} %shard_map.127) | data formatting | bytes 2097152

commit v8 on v7

--- a/solution.py
+++ b/solution.py
@@ -121,17 +121,22 @@
         row = pl.ds(layer, 1)
         norm_rows(state, normed, g1[row, :], s1[row, :], 32)
 
-        for slot, dst in ((0, q_t), (2, v_t)):
-            bias = bqkv[layer, slot].T
-            for start in range(0, width, 512):
-                part = lax.dot_general(wqkv[layer, pl.ds(slot * width + start, 512), :], normed[...], NT, preferred_element_type=F32)
-                for off in range(0, 512, head_dim):
-                    head = (start + off) // head_dim
-                    dst[pl.ds(start + off, head_dim), :] = (part[off:off + head_dim] + bias[:, head:head + 1]).astype(BF)
-        for start in range(0, width, 512):
-            part = lax.dot_general(normed[...], wqkv[layer, pl.ds(width + start, 512), :], NT, preferred_element_type=F32)
-            bias = jnp.concatenate([bqkv[layer, 1, pl.ds((start + off) // head_dim, 1), :] for off in range(0, 512, head_dim)], axis=-1)
-            keys[:, pl.ds(start, 512)] = (part + bias).astype(BF)
+        group = 256
+        group_heads = group // head_dim
+        bias_q, bias_v = bqkv[layer, 0].T, bqkv[layer, 2].T
+
+        def make_rows(slot, bias, dst, index):
+            start = index * group
+            part = lax.dot_general(wqkv[layer, pl.ds(slot * width + start, group), :], normed[...], NT, preferred_element_type=F32)
+            for off in range(0, group, head_dim):
+                head = (start + off) // head_dim
+                dst[pl.ds(start + off, head_dim), :] = (part[off:off + head_dim] + bias[:, head:head + 1]).astype(BF)
+
+        def make_keys(index):
+            start = index * group
+            part = lax.dot_general(normed[...], wqkv[layer, pl.ds(width + start, group), :], NT, preferred_element_type=F32)
+            bias = jnp.concatenate([bqkv[layer, 1, pl.ds((start + off) // head_dim, 1), :] for off in range(0, group, head_dim)], axis=-1)
+            keys[:, pl.ds(start, group)] = (part + bias).astype(BF)
 
         scale = head_dim ** -0.5 / math.log(2.0)
         zeros = jnp.zeros((head_dim, tokens), BF)
@@ -153,10 +158,20 @@
             part = jnp.dot(v_t[pl.ds(head * head_dim, head_dim), :], probs[head % 4], preferred_element_type=F32)
             mixed_t[pl.ds(head * head_dim, head_dim), :] = part * (1.0 / totals[head % 4])
 
+        make_rows(0, bias_q, q_t, 0)
+        make_keys(0)
+        make_rows(2, bias_v, v_t, 0)
         for step in range(0, heads + 4, 2):
             for head in (step, step + 1):
                 if head < heads:
                     score(head)
+            ahead = step // group_heads + 1
+            if ahead * group < width:
+                if step % group_heads == 0:
+                    make_rows(0, bias_q, q_t, ahead)
+                    make_keys(ahead)
+                else:
+                    make_rows(2, bias_v, v_t, ahead)
             for head in (step - 2, step - 1):
                 if 0 <= head < heads:
                     soften(head)
@@ -196,17 +211,25 @@
         def _():
             slot = me * images + image
 
-            for hop in sorted(hops(peers, 0) + hops(peers, 1), key=lambda hop: (-min(hop, peers // 2 - hop), hop)):
+            def give(peer):
+                rows = pl.ds(pl.multiple_of(peer * block, block), block)
+                pltpu.make_async_remote_copy(
+                    src_ref=hid.at[image, rows, :], dst_ref=out_ref.at[slot],
+                    send_sem=out_send, recv_sem=out_recv,
+                    device_id={'sp': peer}, device_id_type=MESH).start()
+
+            for peer in (1, 0):
+                @pl.when(peer != me)
+                def _():
+                    give(peer)
+
+            for hop in sorted(range(peers // 2), key=lambda hop: (-min(hop, peers // 2 - hop), hop)):
                 for core in range(2):
                     peer = 2 * lax.rem(me // 2 + hop, peers // 2) + core
-                    rows = pl.ds(pl.multiple_of(peer * block, block), block)
-
-                    @pl.when(peer != me)
+
+                    @pl.when(jnp.logical_and(peer != me, peer > 1))
                     def _():
-                        pltpu.make_async_remote_copy(
-                            src_ref=hid.at[image, rows, :], dst_ref=out_ref.at[slot],
-                            send_sem=out_send, recv_sem=out_recv,
-                            device_id={'sp': peer}, device_id_type=MESH).start()
+                        give(peer)
 
             out_ref[slot] = hid[image, my_rows, :]
 

time: 75 us -> 73 us (0.973)
  the two profiles are of different devices: /device:TPU:21 before, /device:TPU:53 now
where the time goes in v8:
time: 73 us; the launch traced here: 72.9 us
  Pallas kernels  71.9 us (98%)
  local copies, waits for them, and re-layouts  0.97 us (1%)
    pallas_call x1, Pallas kernels, device_step(): pl.pallas_call(functools.partial(kernel, peers), out_shape=pltpu.VMEM(ima...  71.9 us

profile of v8, /device:TPU:53, one launch (start us, length us, event | category | flops | bytes accessed | tf_op | source)
XLA Modules:
  0.0 72.9 jit_solution(13706146764674840950)
XLA Ops:
  0.0 71.9 %shard_map.127 = bf16[32,16,1024]{2,1,0:T(8,128)(2,1)S(1)} custom-call(bf16[32,16,1024]{2,1,0:T(8,128)(2,1)} %x_ref.1, f32[2,1024]{1,0:T(2,128)} %g1_hbm.1, f32[2,1024]{1,0:T(2,128)} %s1_hbm.1, bf16[2,3072,1024]{2,1,0:T(8,128)(2,1)} %bitcast.4, f32[2,3,16,64]{3,2,1,0:T(8,128)} %bqkv_hbm.1, bf16[2,1024,1024]{2,1,0:T(8,128)(2,1)} %bitcast.5, ...), custom_call_target="tpu_custom_call" | custom-call | tf_op jit(solution)/shard_map/pallas_call | solution.py:261
  71.9 1.0 %copy.15 = bf16[32,16,1024]{2,1,0:T(8,128)(2,1)} copy(bf16[32,16,1024]{2,1,0:T(8,128)(2,1)S(1)} %shard_map.127) | data formatting | bytes 2097152

commit v9 on v8

--- a/solution.py
+++ b/solution.py
@@ -35,6 +35,12 @@
 def hops(peers, parity):
     chips = peers // 2
     return sorted(range(parity, chips, 2), key=lambda hop: (-min(hop, chips - hop), hop))
+
+
+def when(cond):
+    if isinstance(cond, bool):
+        return (lambda run: run()) if cond else (lambda run: None)
+    return pl.when(cond)
 
 
 def kernel(peers, x_ref, g1_hbm, s1_hbm, wqkv_hbm, bqkv_hbm, wout_hbm, bout_hbm, g2_hbm, s2_hbm, wup_hbm, bup_hbm, wdown_hbm, bdown_hbm,
@@ -104,17 +110,18 @@
     for copy in params:
         copy.wait()
 
-    def body(step_idx, carry):
+    def body(step_idx):
+        last = isinstance(step_idx, int)
         image = step_idx // layers
-        layer = lax.rem(step_idx, layers)
+        layer = step_idx % layers if last else lax.rem(step_idx, layers)
         state = hid.at[image]
 
-        @pl.when(image == 0)
+        @when(image == 0)
         def _():
             for copy in weight_copies(layer)[:2]:
                 copy.wait()
 
-        @pl.when(layer == 0)
+        @when(layer == 0)
         def _():
             pltpu.make_async_copy(state, state, in_recv.at[image]).wait()
 
@@ -187,37 +194,26 @@
             part = jnp.dot(mixed[...], wout[layer, :, cols], preferred_element_type=F32) + bout[row, cols]
             state[:, cols] = (state[:, cols].astype(F32) + part).astype(BF)
 
-        @pl.when(image == 0)
+        @when(image == 0)
         def _():
             for copy in weight_copies(layer)[2:]:
                 copy.wait()
 
-        @pl.when(step_idx == 0)
+        @when(step_idx == 0)
         def _():
             for other in range(1, images):
                 send_in(other, False)
 
-        norm_rows(state, normed, g2[row, :], s2[row, :], 32)
-        for start in range(0, mlp_dim, 512):
-            cols = pl.ds(start, 512)
-            part = jnp.dot(normed[...], wup[layer, :, cols], preferred_element_type=F32) + bup[row, cols]
-            active[:, cols] = gelu(part).astype(BF)
-        for start in range(0, width, 512):
-            cols = pl.ds(start, 512)
-            part = jnp.dot(active[...], wdown[layer, :, cols], preferred_element_type=F32) + bdown[row, cols]
-            state[:, cols] = (state[:, cols].astype(F32) + part).astype(BF)
-
-        @pl.when(layer == layers - 1)
-        def _():
-            slot = me * images + image
-
-            def give(peer):
-                rows = pl.ds(pl.multiple_of(peer * block, block), block)
-                pltpu.make_async_remote_copy(
-                    src_ref=hid.at[image, rows, :], dst_ref=out_ref.at[slot],
-                    send_sem=out_send, recv_sem=out_recv,
-                    device_id={'sp': peer}, device_id_type=MESH).start()
-
+        slot = me * images + image
+
+        def give(peer):
+            rows = pl.ds(pl.multiple_of(peer * block, block), block)
+            pltpu.make_async_remote_copy(
+                src_ref=hid.at[image, rows, :], dst_ref=out_ref.at[slot],
+                send_sem=out_send, recv_sem=out_recv,
+                device_id={'sp': peer}, device_id_type=MESH).start()
+
+        def leave():
             for peer in (1, 0):
                 @pl.when(peer != me)
                 def _():
@@ -233,9 +229,71 @@
 
             out_ref[slot] = hid[image, my_rows, :]
 
-        return carry
-
-    lax.fori_loop(0, images * layers, body, 0)
+        def leave_part(part):
+            count = peers // 4
+            for turn in range(count):
+                index = lax.rem(me // 2 + turn, count)
+                chip = index // (count // 2) * count + part * (count // 2) + lax.rem(index, count // 2)
+                for core in range(2):
+                    peer = 2 * chip + core
+
+                    @pl.when(peer != me)
+                    def _():
+                        give(peer)
+
+            @pl.when(lax.rem(me // count, 2) == part)
+            def _():
+                out_ref[slot] = hid[image, my_rows, :]
+
+        if last:
+            quarter = tokens // 4
+
+            def norm_part(part):
+                for index in range(2):
+                    norm_rows(state.at[pl.ds((2 * index + part) * quarter, quarter), :],
+                              normed.at[pl.ds((2 * part + index) * quarter, quarter), :], g2[row, :], s2[row, :], 32)
+
+            def widen_part(part):
+                rows = pl.ds(2 * part * quarter, 2 * quarter)
+                for start in range(0, mlp_dim, 512):
+                    cols = pl.ds(start, 512)
+                    part_up = jnp.dot(normed[rows, :], wup[layer, :, cols], preferred_element_type=F32) + bup[row, cols]
+                    active[rows, cols] = gelu(part_up).astype(BF)
+
+            def narrow_part(part):
+                for start in range(0, width, 512):
+                    cols = pl.ds(start, 512)
+                    part_down = jnp.dot(active[pl.ds(2 * part * quarter, 2 * quarter), :], wdown[layer, :, cols], preferred_element_type=F32) + bdown[row, cols]
+                    for index in range(2):
+                        rows = pl.ds((2 * index + part) * quarter, quarter)
+                        state[rows, cols] = (state[rows, cols].astype(F32) + part_down[index * quarter:(index + 1) * quarter]).astype(BF)
+
+            norm_part(0)
+            widen_part(0)
+            norm_part(1)
+            narrow_part(0)
+            leave_part(0)
+            widen_part(1)
+            narrow_part(1)
+            leave_part(1)
+        else:
+            norm_rows(state, normed, g2[row, :], s2[row, :], 32)
+            for start in range(0, mlp_dim, 512):
+                cols = pl.ds(start, 512)
+                part = jnp.dot(normed[...], wup[layer, :, cols], preferred_element_type=F32) + bup[row, cols]
+                active[:, cols] = gelu(part).astype(BF)
+            for start in range(0, width, 512):
+                cols = pl.ds(start, 512)
+                part = jnp.dot(active[...], wdown[layer, :, cols], preferred_element_type=F32) + bdown[row, cols]
+                state[:, cols] = (state[:, cols].astype(F32) + part).astype(BF)
+
+            pl.when(layer == layers - 1)(leave)
+
+    @pl.loop(0, images * layers - 1)
+    def _(step_idx):
+        body(step_idx)
+
+    body(images * layers - 1)
 
     sent = x_ref.at[pl.ds(0, (peers - 1) * images)]
     pltpu.make_async_copy(sent, sent, in_send).wait()

time: 73 us -> 71.9 us (0.985)
  the two profiles are of different devices: /device:TPU:53 before, /device:TPU:93 now
where the time goes in v9:
time: 71.9 us
  Pallas kernels  70.9 us (99%)
  local copies, waits for them, and re-layouts  0.97 us (1%)
    pallas_call x1, Pallas kernels, device_step(): pl.pallas_call(functools.partial(kernel, peers), out_shape=pltpu.VMEM(ima...  70.9 us

profile of v9, /device:TPU:93, one launch (start us, length us, event | category | flops | bytes accessed | tf_op | source)
XLA Modules:
  0.0 71.9 jit_solution(2772585365878647659)
XLA Ops:
  0.0 70.9 %shard_map.127 = bf16[32,16,1024]{2,1,0:T(8,128)(2,1)S(1)} custom-call(bf16[32,16,1024]{2,1,0:T(8,128)(2,1)} %x_ref.1, f32[2,1024]{1,0:T(2,128)} %g1_hbm.1, f32[2,1024]{1,0:T(2,128)} %s1_hbm.1, bf16[2,3072,1024]{2,1,0:T(8,128)(2,1)} %bitcast.4, f32[2,3,16,64]{3,2,1,0:T(8,128)} %bqkv_hbm.1, bf16[2,1024,1024]{2,1,0:T(8,128)(2,1)} %bitcast.5, ...), custom_call_target="tpu_custom_call" | custom-call | tf_op jit(solution)/shard_map/pallas_call | solution.py:319
  70.9 1.0 %copy.15 = bf16[32,16,1024]{2,1,0:T(8,128)(2,1)} copy(bf16[32,16,1024]{2,1,0:T(8,128)(2,1)S(1)} %shard_map.127) | data formatting | bytes 2097152

commit v10 on v9

--- a/solution.py
+++ b/solution.py
@@ -207,7 +207,7 @@
         slot = me * images + image
 
         def give(peer):
-            rows = pl.ds(pl.multiple_of(peer * block, block), block)
+            rows = pl.ds(peer * block, block) if isinstance(peer, int) else pl.ds(pl.multiple_of(peer * block, block), block)
             pltpu.make_async_remote_copy(
                 src_ref=hid.at[image, rows, :], dst_ref=out_ref.at[slot],
                 send_sem=out_send, recv_sem=out_recv,
@@ -229,11 +229,13 @@
 
             out_ref[slot] = hid[image, my_rows, :]
 
+        chip_rows = 2 * block
+        chips = peers // 2
+        early = (0, chips - 2) + tuple(range(1, chips // 2 - 1))
+        parts = (early, (chips // 2 - 1,) + tuple(chip for chip in reversed(range(chips)) if chip not in early + (chips // 2 - 1,)))
+
         def leave_part(part):
-            count = peers // 4
-            for turn in range(count):
-                index = lax.rem(me // 2 + turn, count)
-                chip = index // (count // 2) * count + part * (count // 2) + lax.rem(index, count // 2)
+            for chip in parts[part]:
                 for core in range(2):
                     peer = 2 * chip + core
 
@@ -241,20 +243,20 @@
                     def _():
                         give(peer)
 
-            @pl.when(lax.rem(me // count, 2) == part)
-            def _():
-                out_ref[slot] = hid[image, my_rows, :]
+                    @pl.when(peer == me)
+                    def _():
+                        out_ref[slot] = hid[image, my_rows, :]
 
         if last:
-            quarter = tokens // 4
+            half = tokens // 2
 
             def norm_part(part):
-                for index in range(2):
-                    norm_rows(state.at[pl.ds((2 * index + part) * quarter, quarter), :],
-                              normed.at[pl.ds((2 * part + index) * quarter, quarter), :], g2[row, :], s2[row, :], 32)
+                for index, chip in enumerate(parts[part]):
+                    norm_rows(state.at[pl.ds(chip * chip_rows, chip_rows), :],
+                              normed.at[pl.ds(part * half + index * chip_rows, chip_rows), :], g2[row, :], s2[row, :], 32)
 
             def widen_part(part):
-                rows = pl.ds(2 * part * quarter, 2 * quarter)
+                rows = pl.ds(part * half, half)
                 for start in range(0, mlp_dim, 512):
                     cols = pl.ds(start, 512)
                     part_up = jnp.dot(normed[rows, :], wup[layer, :, cols], preferred_element_type=F32) + bup[row, cols]
@@ -263,10 +265,10 @@
             def narrow_part(part):
                 for start in range(0, width, 512):
                     cols = pl.ds(start, 512)
-                    part_down = jnp.dot(active[pl.ds(2 * part * quarter, 2 * quarter), :], wdown[layer, :, cols], preferred_element_type=F32) + bdown[row, cols]
-                    for index in range(2):
-                        rows = pl.ds((2 * index + part) * quarter, quarter)
-                        state[rows, cols] = (state[rows, cols].astype(F32) + part_down[index * quarter:(index + 1) * quarter]).astype(BF)
+                    part_down = jnp.dot(active[pl.ds(part * half, half), :], wdown[layer, :, cols], preferred_element_type=F32) + bdown[row, cols]
+                    for index, chip in enumerate(parts[part]):
+                        rows = pl.ds(chip * chip_rows, chip_rows)
+                        state[rows, cols] = (state[rows, cols].astype(F32) + part_down[index * chip_rows:(index + 1) * chip_rows]).astype(BF)
 
             norm_part(0)
             widen_part(0)

time: 71.9 us -> 71.9 us (level)
  the two profiles are of different devices: /device:TPU:93 before, /device:TPU:21 now
where the time goes in v10:
time: 71.9 us; the launch traced here: 71.8 us
  Pallas kernels  70.8 us (98%)
  local copies, waits for them, and re-layouts  0.97 us (1%)
    pallas_call x1, Pallas kernels, device_step(): pl.pallas_call(functools.partial(kernel, peers), out_shape=pltpu.VMEM(ima...  70.8 us

profile of v10, /device:TPU:21, one launch (start us, length us, event | category | flops | bytes accessed | tf_op | source)
XLA Modules:
  0.0 71.8 jit_solution(54071710978169086)
XLA Ops:
  0.0 70.8 %shard_map.127 = bf16[32,16,1024]{2,1,0:T(8,128)(2,1)S(1)} custom-call(bf16[32,16,1024]{2,1,0:T(8,128)(2,1)} %x_ref.1, f32[2,1024]{1,0:T(2,128)} %g1_hbm.1, f32[2,1024]{1,0:T(2,128)} %s1_hbm.1, bf16[2,3072,1024]{2,1,0:T(8,128)(2,1)} %bitcast.4, f32[2,3,16,64]{3,2,1,0:T(8,128)} %bqkv_hbm.1, bf16[2,1024,1024]{2,1,0:T(8,128)(2,1)} %bitcast.5, ...), custom_call_target="tpu_custom_call" | custom-call | tf_op jit(solution)/shard_map/pallas_call | solution.py:321
  70.8 1.0 %copy.15 = bf16[32,16,1024]{2,1,0:T(8,128)(2,1)} copy(bf16[32,16,1024]{2,1,0:T(8,128)(2,1)S(1)} %shard_map.127) | data formatting | bytes 2097152

commit v11 on v10

--- a/solution.py
+++ b/solution.py
@@ -231,12 +231,12 @@
 
         chip_rows = 2 * block
         chips = peers // 2
-        early = (0, chips - 2) + tuple(range(1, chips // 2 - 1))
+        early = tuple(range(chips // 2 - 1)) + (chips - 2,)
         parts = (early, (chips // 2 - 1,) + tuple(chip for chip in reversed(range(chips)) if chip not in early + (chips // 2 - 1,)))
 
         def leave_part(part):
             for chip in parts[part]:
-                for core in range(2):
+                for core in (1, 0):
                     peer = 2 * chip + core
 
                     @pl.when(peer != me)

time: 71.9 us -> 71.9 us (level)
  no operation moved by 1% of the time
where the time goes in v11:
time: 71.9 us; the launch traced here: 71.8 us
  Pallas kernels  70.8 us (98%)
  local copies, waits for them, and re-layouts  0.97 us (1%)
    pallas_call x1, Pallas kernels, device_step(): pl.pallas_call(functools.partial(kernel, peers), out_shape=pltpu.VMEM(ima...  70.8 us

profile of v11, /device:TPU:21, one launch (start us, length us, event | category | flops | bytes accessed | tf_op | source)
XLA Modules:
  0.0 71.8 jit_solution(6284359000845270136)
XLA Ops:
  0.0 70.8 %shard_map.127 = bf16[32,16,1024]{2,1,0:T(8,128)(2,1)S(1)} custom-call(bf16[32,16,1024]{2,1,0:T(8,128)(2,1)} %x_ref.1, f32[2,1024]{1,0:T(2,128)} %g1_hbm.1, f32[2,1024]{1,0:T(2,128)} %s1_hbm.1, bf16[2,3072,1024]{2,1,0:T(8,128)(2,1)} %bitcast.4, f32[2,3,16,64]{3,2,1,0:T(8,128)} %bqkv_hbm.1, bf16[2,1024,1024]{2,1,0:T(8,128)(2,1)} %bitcast.5, ...), custom_call_target="tpu_custom_call" | custom-call | tf_op jit(solution)/shard_map/pallas_call | solution.py:321
  70.8 1.0 %copy.15 = bf16[32,16,1024]{2,1,0:T(8,128)(2,1)} copy(bf16[32,16,1024]{2,1,0:T(8,128)(2,1)S(1)} %shard_map.127) | data formatting | bytes 2097152

commit v12 on v11

--- a/solution.py
+++ b/solution.py
@@ -118,12 +118,19 @@
 
         @when(image == 0)
         def _():
-            for copy in weight_copies(layer)[:2]:
+            for copy in weight_copies(layer):
                 copy.wait()
 
         @when(layer == 0)
         def _():
             pltpu.make_async_copy(state, state, in_recv.at[image]).wait()
+
+        final_wave = lax.rem(me, 4) == 3
+
+        @when(False if last else jnp.logical_or(jnp.logical_and(step_idx == 0, final_wave), jnp.logical_and(step_idx == 1, jnp.logical_not(final_wave))))
+        def _():
+            for other in range(1, images):
+                send_in(other, False)
 
         row = pl.ds(layer, 1)
         norm_rows(state, normed, g1[row, :], s1[row, :], 32)
@@ -193,16 +200,6 @@
             cols = pl.ds(start, 512)
             part = jnp.dot(mixed[...], wout[layer, :, cols], preferred_element_type=F32) + bout[row, cols]
             state[:, cols] = (state[:, cols].astype(F32) + part).astype(BF)
-
-        @when(image == 0)
-        def _():
-            for copy in weight_copies(layer)[2:]:
-                copy.wait()
-
-        @when(step_idx == 0)
-        def _():
-            for other in range(1, images):
-                send_in(other, False)
 
         slot = me * images + image
 

time: 71.9 us -> 73.6 us (1.024)
  Pallas kernels: 70.8 us -> 72.6 us
    pallas_call x1, Pallas kernels: 70.8 us -> 72.6 us  [device_step(): pl.pallas_call(functools.partial(kernel, peers), out_shape=pltpu.VMEM(ima...]
where the time goes in v12:
time: 73.6 us
  Pallas kernels  72.6 us (99%)
  local copies, waits for them, and re-layouts  0.97 us (1%)
    pallas_call x1, Pallas kernels, device_step(): pl.pallas_call(functools.partial(kernel, peers), out_shape=pltpu.VMEM(ima...  72.6 us

profile of v12, /device:TPU:21, one launch (start us, length us, event | category | flops | bytes accessed | tf_op | source)
XLA Modules:
  0.0 73.6 jit_solution(14546225391133096894)
XLA Ops:
  0.0 72.6 %shard_map.127 = bf16[32,16,1024]{2,1,0:T(8,128)(2,1)S(1)} custom-call(bf16[32,16,1024]{2,1,0:T(8,128)(2,1)} %x_ref.1, f32[2,1024]{1,0:T(2,128)} %g1_hbm.1, f32[2,1024]{1,0:T(2,128)} %s1_hbm.1, bf16[2,3072,1024]{2,1,0:T(8,128)(2,1)} %bitcast.4, f32[2,3,16,64]{3,2,1,0:T(8,128)} %bqkv_hbm.1, bf16[2,1024,1024]{2,1,0:T(8,128)(2,1)} %bitcast.5, ...), custom_call_target="tpu_custom_call" | custom-call | tf_op jit(solution)/shard_map/pallas_call | solution.py:318
  72.6 1.0 %copy.15 = bf16[32,16,1024]{2,1,0:T(8,128)(2,1)} copy(bf16[32,16,1024]{2,1,0:T(8,128)(2,1)S(1)} %shard_map.127) | data formatting | bytes 2097152

commit v13 on v11

--- a/solution.py
+++ b/solution.py
@@ -65,7 +65,7 @@
     my_rows = pl.ds(pl.multiple_of(me * block, block), block)
 
     def send_in(image, ask):
-        for core in range(2):
+        for core in (1, 0):
             for parity in range(2):
                 odd = lax.rem(me // 2 + parity, 2)
                 for even_hop, odd_hop in zip(hops(peers, 0), hops(peers, 1)):

time: 71.9 us -> 70 us (0.974); the launches traced: 71.8 us -> 69 us
  Pallas kernels: 70.8 us -> 68 us
    pallas_call x1, Pallas kernels: 70.8 us -> 68 us  [device_step(): pl.pallas_call(functools.partial(kernel, peers), out_shape=pltpu.VMEM(ima...]
where the time goes in v13:
time: 70 us; the launch traced here: 69 us
  Pallas kernels  68 us (97%)
  local copies, waits for them, and re-layouts  0.97 us (1%)
    pallas_call x1, Pallas kernels, device_step(): pl.pallas_call(functools.partial(kernel, peers), out_shape=pltpu.VMEM(ima...  68 us

profile of v13, /device:TPU:21, one launch (start us, length us, event | category | flops | bytes accessed | tf_op | source)
XLA Modules:
  0.0 69.0 jit_solution(8444198241026558277)
XLA Ops:
  0.0 68.0 %shard_map.127 = bf16[32,16,1024]{2,1,0:T(8,128)(2,1)S(1)} custom-call(bf16[32,16,1024]{2,1,0:T(8,128)(2,1)} %x_ref.1, f32[2,1024]{1,0:T(2,128)} %g1_hbm.1, f32[2,1024]{1,0:T(2,128)} %s1_hbm.1, bf16[2,3072,1024]{2,1,0:T(8,128)(2,1)} %bitcast.4, f32[2,3,16,64]{3,2,1,0:T(8,128)} %bqkv_hbm.1, bf16[2,1024,1024]{2,1,0:T(8,128)(2,1)} %bitcast.5, ...), custom_call_target="tpu_custom_call" | custom-call | tf_op jit(solution)/shard_map/pallas_call | solution.py:321
  68.0 1.0 %copy.15 = bf16[32,16,1024]{2,1,0:T(8,128)(2,1)} copy(bf16[32,16,1024]{2,1,0:T(8,128)(2,1)S(1)} %shard_map.127) | data formatting | bytes 2097152
